TPU v7x, 8 devices: a whole 2x2x1 slice. The times are simulated.
8 devices in a mesh: data: 2 (over z, y), tp: 4 (over x, core).
Axes of the slice: x: 2, y: 2, z: 1, core: 2. Of those that a mesh axis runs over, the one named last changes fastest.
Arguments:
- x: bfloat16 [2048, 49152], P('data', 'tp'), parts along dimension 0
- w: bfloat16 [49152, 12288], P('tp')
- lengths: int32 [8], P('data'), parts along dimension 0
Outputs:
- output: bfloat16 [2048, 12288], P('data'), parts along dimension 0
There are 2 independent parts. A program takes and returns all parts, laid end to end along the dimension named above; an argument that names none is the same for every part.
All inputs are finite; a program needn't handle non-finite values.
Results may differ from a plain program's by a relative error of at most 0.001.
Values are sent between devices in bfloat16 or wider.
A program may use at most 1.5 GiB of HBM per device.

v0:
```python
import functools

import jax
import jax.numpy as jnp
from jax import lax
from jax.experimental import pallas as pl
from jax.experimental.pallas import tpu as pltpu
from jax.sharding import PartitionSpec as P

MESH = pl.DeviceIdType.MESH
TILE = 16
NB = 256
HB = NB // 2
KC = 3072
BUCKETS = (352, 416, 448) + tuple(range(480, 673, 16)) + (704, 736, 784)
PER = 2
LAST = 7
OFFS, LONE_TILE, LONE_ROW, LONE_SLOT, LONE_SOURCE, MERGE = 50, 54, 55, 56, 57, 64


def fused_kernel(rows, table_ref, x_ref, w_ref, y_ref, xp, stage0, stage1, lone, wbuf, part, ra, sb, so, rb, out,
                 xsem, wsem, send_a, recv_a, send_b, recv_b, send_c, recv_c, send_e, recv_e, send_d, recv_d, osem):
    depth, cols = w_ref.shape
    blocks = cols // NB
    half = rows // 2
    stages = (stage0, stage1)
    me = lax.axis_index("tp")
    core = lax.rem(me, 2)
    chip = me // 2
    sibling = {"tp": me + 1 - 2 * core}
    peer = {"tp": lax.rem(me + 2, 4)}
    nk = depth // KC

    def x_copy(k):
        return pltpu.make_async_copy(x_ref.at[:, :, pl.ds(k * KC, KC)], stages[k % 2], xsem.at[k % 2])

    def w_copy(b, k):
        s = lax.rem(b, 2)
        deep = pl.ds(pl.multiple_of(k * KC, KC), KC)
        return pltpu.make_async_copy(w_ref.at[deep, pl.ds(pl.multiple_of(b * NB, NB), NB)], wbuf.at[s, deep], wsem.at[s, k])

    def remote(src, dst, ssem, rsem, to):
        return pltpu.make_async_remote_copy(src_ref=src, dst_ref=dst, send_sem=ssem, recv_sem=rsem, device_id=to, device_id_type=MESH)

    def copy_a(b):
        s = lax.rem(b, 2)
        return remote(part.at[s, 1 - core], ra.at[s], send_a.at[s], recv_a.at[s], sibling)

    def copy_b(b):
        s, r = lax.rem(b, 4), lax.rem(b, 8)
        return remote(sb.at[s], rb.at[r], send_b.at[s], recv_b.at[r], peer)

    def copy_c(b):
        r = lax.rem(b, 8)
        return remote(out.at[r, core, chip], out.at[r, core, chip], send_c.at[r], recv_c.at[r], peer)

    def copy_e(b):
        r = lax.rem(b, 8)
        return remote(out.at[r, core, chip], out.at[r, core, chip], send_e.at[r], recv_e.at[r], sibling)

    def copy_d(b):
        r = lax.rem(b, 8)
        return remote(out.at[r, core, 1 - chip], out.at[r, core, 1 - chip], send_d.at[r], recv_d.at[r], sibling)

    def copy_o(b):
        r = lax.rem(b, 8)
        return pltpu.make_async_copy(out.at[r], y_ref.at[b], osem.at[r])

    x_copy(0).start()
    w_copy(0, 0).start()
    x_copy(1).start()
    w_copy(0, 1).start()

    barrier = pltpu.get_barrier_semaphore()
    for other in (sibling, peer):
        pl.semaphore_signal(barrier, inc=1, device_id=other, device_id_type=MESH)
    pl.semaphore_wait(barrier, 2)

    row = lax.broadcasted_iota(jnp.int32, (TILE, KC), 0)

    def pack(k):
        stage = stages[k % 2]
        x_copy(k).wait()
        first = stage[table_ref[LONE_SOURCE]][0:1, :].astype(jnp.float32)
        lone[...] = jnp.broadcast_to(first, (TILE, KC)).astype(lone.dtype)

        def tile(t, carry):
            at = pl.ds(pl.multiple_of(t * TILE, TILE), TILE)
            xp[at, k * KC:(k + 1) * KC] = jnp.where(row + 1 == table_ref[MERGE + t], lone[...], stage[table_ref[t]])
            return carry

        lax.fori_loop(0, rows // TILE, tile, 0)
        if k + 2 < nk:
            x_copy(k + 2).start()
            w_copy(0, k + 2).start()
        if k == nk - 1:
            for j in range(nk):
                w_copy(1, j).start()

    def exchange(i):
        @pl.when(jnp.logical_and(i >= 1, i - 1 < blocks))
        def _():
            b = i - 1
            s, q = lax.rem(b, 2), lax.rem(b, 4)
            copy_a(b).wait()
            there = pl.ds(pl.multiple_of((1 - chip) * half, 8), half)
            here = pl.ds(pl.multiple_of(chip * half, 8), half)
            sb[q] = part[s, core, there, :] + ra[s, there, :]
            so[q] = part[s, core, here, :] + ra[s, here, :]
            copy_b(b).start()

        @pl.when(jnp.logical_and(i >= 3, i - 3 < blocks))
        def _():
            b = i - 3
            copy_b(b).wait()
            out[lax.rem(b, 8), core, chip] = (so[lax.rem(b, 4)] + rb[lax.rem(b, 8)]).astype(out.dtype)
            copy_c(b).start()
            copy_e(b).start()

        @pl.when(jnp.logical_and(i >= 5, i - 5 < blocks))
        def _():
            copy_c(i - 5).wait()
            copy_d(i - 5).start()

        @pl.when(jnp.logical_and(i >= 6, i - 6 < blocks))
        def _():
            copy_e(i - 6).wait()
            copy_d(i - 6).wait()
            copy_o(i - 6).start()

        @pl.when(jnp.logical_and(i >= 7, i - 7 < blocks))
        def _():
            copy_o(i - 7).wait()

    def step(j, carry):
        i, k = j // nk, lax.rem(j, nk)
        for early in range(nk):
            pl.when(j == early)(functools.partial(pack, early))

        @pl.when(k == jnp.where(i == 1, 1, 2))
        def _():
            exchange(i)

        @pl.when(i < blocks)
        def _():
            @pl.when(jnp.logical_and(i >= 1, i + 1 < blocks))
            def _():
                w_copy(i + 1, k).start()

            w_copy(i, k).wait()
            s = lax.rem(i, 2)
            deep = pl.ds(pl.multiple_of(k * KC, KC), KC)
            prod = jnp.dot(xp[:, deep], wbuf[s, deep, :], preferred_element_type=jnp.float32)
            for h in range(2):
                part[s, h] = jnp.where(k == 0, 0.0, part[s, h]) + prod[:, h * HB:(h + 1) * HB]

            @pl.when(k == nk - 1)
            def _():
                copy_a(i).start()

        return carry

    lax.fori_loop(0, nk * (blocks + LAST), step, 0)


def unpack_kernel(lens_ref, table_ref, p_ref, y_ref, packed, spread, isem, osem):
    slots = lens_ref.shape[0]
    chunks, tokens, width = spread.shape
    slot_tiles = tokens // slots // TILE
    row = lax.broadcasted_iota(jnp.int32, (TILE, HB), 0)

    def fetch(c):
        return pltpu.make_async_copy(p_ref.at[pl.ds(c * PER, PER)], packed.at[c], isem.at[c])

    def store(c):
        return pltpu.make_async_copy(spread.at[c], y_ref.at[:, pl.ds(pl.multiple_of(c * width, width), width)], osem.at[c])

    def chunk(c, carry):
        fetch(c).wait()

        def move(source, target, count, length=None):
            source = pl.multiple_of(source * TILE, TILE)
            target = pl.multiple_of(target * TILE, TILE)
            for j in range(width // HB):
                piece = packed[c, j // 2, j % 2, pl.ds(source, count * TILE), :]
                if length is not None:
                    piece = jnp.where(row < length, piece, jnp.zeros_like(piece))
                spread[c, pl.ds(target, count * TILE), j * HB:(j + 1) * HB] = piece

        def clear(target, count):
            at = pl.ds(pl.multiple_of(target * TILE, TILE), count * TILE)
            spread[c, at, :] = jnp.zeros((count * TILE, width), spread.dtype)

        for s in range(slots):
            merged = jnp.logical_and(table_ref[LONE_TILE] > 0, table_ref[LONE_SLOT] == s)
            length = jnp.where(merged, 0, lens_ref[s])
            full = lax.div(length, TILE)
            used = lax.div(length + TILE - 1, TILE)
            source, target = table_ref[OFFS + s], s * slot_tiles
            quads = lax.div(full, 4)
            empty = lax.div(used + 3, 4)

            @pl.loop(0, quads)
            def _(t, source=source, target=target):
                move(source + 4 * t, target + 4 * t, 4)

            @pl.loop(quads * 4, full)
            def _(t, source=source, target=target):
                move(source + t, target + t, 1)

            @pl.when(full < used)
            def _(source=source, target=target, full=full, length=length):
                move(source + full, target + full, 1, length - full * TILE)

            @pl.loop(used, empty * 4)
            def _(t, target=target):
                clear(target + t, 1)

            @pl.loop(empty, slot_tiles // 4)
            def _(t, target=target):
                clear(target + 4 * t, 4)

        @pl.when(table_ref[LONE_TILE] > 0)
        def _():
            source = pl.multiple_of((table_ref[LONE_TILE] - 1) * TILE, TILE)
            target = pl.multiple_of(table_ref[LONE_SLOT] * (slot_tiles * TILE), TILE)
            for j in range(width // HB):
                piece = packed[c, j // 2, j % 2, pl.ds(source, TILE), :].astype(jnp.float32)
                line = jnp.sum(jnp.where(row == table_ref[LONE_ROW], piece, 0.0), axis=0, keepdims=True)
                spread[c, pl.ds(target, TILE), j * HB:(j + 1) * HB] = jnp.where(row == 0, line, 0.0).astype(spread.dtype)

        store(c).start()
        return carry

    for c in range(chunks):
        fetch(c).start()
    lax.fori_loop(0, chunks, chunk, 0)
    for c in range(chunks):
        store(c).wait()


def branch(index, rows, x_loc, w_loc, lengths, table):
    tokens, depth = x_loc.shape
    cols = w_loc.shape[1]
    blocks = cols // NB
    half = rows // 2
    f32, bf16 = jnp.float32, x_loc.dtype
    dma = pltpu.SemaphoreType.DMA
    packed = pl.pallas_call(
        functools.partial(fused_kernel, rows),
        out_shape=jax.ShapeDtypeStruct((blocks, 2, 2, half, HB), bf16),
        in_specs=[pl.BlockSpec(memory_space=pltpu.SMEM), pl.BlockSpec(memory_space=pl.ANY), pl.BlockSpec(memory_space=pl.ANY)],
        out_specs=pl.BlockSpec(memory_space=pl.ANY),
        scratch_shapes=[
            pltpu.VMEM((rows, depth), bf16),
            pltpu.VMEM((tokens // TILE, TILE, KC), bf16),
            pltpu.VMEM((tokens // TILE, TILE, KC), bf16),
            pltpu.VMEM((TILE, KC), bf16),
            pltpu.VMEM((2, depth, NB), bf16),
            pltpu.VMEM((2, 2, rows, HB), f32),
            pltpu.VMEM((2, rows, HB), f32),
            pltpu.VMEM((4, half, HB), f32),
            pltpu.VMEM((4, half, HB), f32),
            pltpu.VMEM((8, half, HB), f32),
            pltpu.VMEM((8, 2, 2, half, HB), bf16),
            dma((2,)), dma((2, depth // KC)), dma((2,)), dma((2,)), dma((4,)), dma((8,)),
            dma((8,)), dma((8,)), dma((8,)), dma((8,)), dma((8,)), dma((8,)), dma((8,)),
        ],
        compiler_params=pltpu.CompilerParams(collective_id=index, has_side_effects=True, vmem_limit_bytes=66_000_000),
        cost_estimate=pl.CostEstimate(flops=2 * rows * depth * cols, bytes_accessed=2 * depth * cols, transcendentals=0),
        name=f"fused_{rows}",
    )(table, x_loc.reshape(tokens // TILE, TILE, depth), w_loc)
    packed = packed.reshape(blocks, 2, rows, HB)
    chunks = blocks // PER
    return pl.pallas_call(
        unpack_kernel,
        out_shape=jax.ShapeDtypeStruct((tokens, cols), bf16),
        in_specs=[pl.BlockSpec(memory_space=pltpu.SMEM), pl.BlockSpec(memory_space=pltpu.SMEM), pl.BlockSpec(memory_space=pl.ANY)],
        out_specs=pl.BlockSpec(memory_space=pl.ANY),
        scratch_shapes=[
            pltpu.VMEM((chunks, PER, 2, rows, HB), bf16),
            pltpu.VMEM((chunks, tokens, PER * NB), bf16),
            dma((chunks,)), dma((chunks,)),
        ],
        compiler_params=pltpu.CompilerParams(vmem_limit_bytes=66_000_000),
        cost_estimate=pl.CostEstimate(flops=0, bytes_accessed=2 * (rows + tokens) * cols, transcendentals=0),
        name=f"unpack_{rows}",
    )(lengths, table, packed)


def make_table(lengths, tokens):
    slots = lengths.shape[0]
    slot_tiles = tokens // slots // TILE
    slot = jnp.arange(slots, dtype=jnp.int32)
    ahead = slot[None, :] < slot[:, None]

    def first(flags):
        return flags & ~jnp.any(ahead & flags[None, :], axis=1)

    lone = first(lengths == 1)
    rest = lax.rem(lengths, TILE)
    free = (rest != 0) & ~lone
    host = first(free)
    merged = lone & jnp.any(free[None, :] & (slot[:, None] >= 0), axis=1)
    tiles = jnp.where(merged, 0, lax.div(lengths + (TILE - 1), TILE))
    offs = jnp.sum(jnp.where(ahead, tiles[None, :], 0), axis=1)
    ends = offs + tiles
    place = jnp.arange(128, dtype=jnp.int32)[:, None]
    cells = jnp.where((place >= offs) & (place < ends), slot * slot_tiles + place - offs, 0)
    cells += jnp.where(place == OFFS + slot, offs, 0)
    cells += jnp.where((place == LONE_TILE) & host, ends, 0)
    cells += jnp.where((place == LONE_ROW) & host, rest, 0)
    cells += jnp.where((place == LONE_SLOT) & lone, slot, 0)
    cells += jnp.where((place == LONE_SOURCE) & lone, slot * slot_tiles, 0)
    cells += jnp.where((place - MERGE == ends - 1) & host, rest + 1, 0)
    return jnp.sum(cells, axis=1), jnp.sum(tiles)


def solution(mesh):
    def local_part(x_loc, w_loc, lengths):
        table, total = make_table(lengths, x_loc.shape[0])
        index = jnp.sum((total * TILE > jnp.array(BUCKETS[:-1], jnp.int32)).astype(jnp.int32))
        return lax.switch(index, [functools.partial(branch, j, rows) for j, rows in enumerate(BUCKETS)], x_loc, w_loc, lengths, table)

    return jax.shard_map(local_part, mesh=mesh, in_specs=(P("data", "tp"), P("tp", None), P("data")), out_specs=P("data", None), check_vma=False)
```

profile of v0, /device:TPU:0, one launch (start us, length us, event | category | flops | bytes accessed | tf_op | source)
XLA Modules:
  0.0 267.7 jit_solution(122968181055569227)
XLA Ops:
  0.0 0.7 broadcast_compare_fusion.76
  0.7 0.1 fusion.154
  0.8 0.1 add.56
  0.9 1.3 fusion.160
  2.2 0.1 fusion.155
  2.3 0.1 and.51
  2.4 0.1 and.108
  2.5 1.9 fusion.159
  5.0 1.3 fusion.156
  6.9 0.1 select_reduce_fusion
  7.0 0.1 ge.21
  7.1 0.1 lt.39
  7.2 260.3 %conditional.1 = (bf16[1024,12288]{1,0:T(8,128)(2,1)}) conditional(s32[]{:T(128)} %clamp.3, (bf16[1024,12288]{1,0:T(8,128)(2,1)}, s32[128,4]{0,1:T(4,128)S(1)}, bf16[12288,12288]{1,0:T(8,128)(2,1)}, s32[4]{0:T(128)}, s32[]{:T(128)}, /*index=5*/s32[128]{0:T(128)S(1)}, s32[128]{0:T(128)S(1)}, s32[4]{0:T(128)S(1)}, ...), branch_computations={%region_7.8_spmd.clone, %region_8.9_spmd.clone, %region_9.10_spmd.... | conditional | flops 236760088576 | bytes 346450176 | solution.py:323
  7.5 0.6 fusion.71.table_ref
  8.1 0.0 copy-start.8
  8.1 245.4 %fused_560.1 = bf16[48,2,2,280,128]{4,3,2,1,0:T(8,128)(2,1)} custom-call(s32[128]{0:T(128)} %fusion.71.table_ref, bf16[64,16,12288]{2,1,0:T(8,128)(2,1)} %bitcast.65, bf16[12288,12288]{1,0:T(8,128)(2,1)} %get-tuple-element.2574.w_ref), custom_call_target="tpu_custom_call" | custom-call | flops 169114337280 | bytes 301989888 | tf_op jit(solution)/shard_map/cond/branch_8_fun/fused_560/pallas_call | solution.py:249
  253.5 0.0 copy-done.8
  253.6 13.4 %unpack_560.1 = bf16[1024,12288]{1,0:T(8,128)(2,1)} custom-call(s32[4]{0:T(128)S(1)} %copy-done.8, s32[128]{0:T(128)} %fusion.71.table_ref, bf16[48,2,560,128]{3,2,1,0:T(8,128)(2,1)} %bitcast.48), custom_call_target="tpu_custom_call" | custom-call | bytes 38928384 | tf_op jit(solution)/shard_map/cond/branch_8_fun/unpack_560/pallas_call | solution.py:275
  (14 shorter events, 0.1 us)
Async XLA Ops:
  8.1 245.4 %copy-start.8 = (s32[4]{0:T(128)S(1)}, s32[4]{0:T(128)}, u32[]{:S(2)}) copy-start(s32[4]{0:T(128)} %get-tuple-element.2571.lens_ref) | copy-start | bytes 52 | tf_op jit(solution)/shard_map/cond
where the time goes:
time: 271 us; the launch traced here: 268 us
  Pallas kernels  259 us (96%)
  other arithmetic  6.2 us (2%)
    pallas_call x1, Pallas kernels, branch(): pl.pallas_call(functools.partial(fused_kernel, rows), out_shape=jax.Shape...  245 us
    pallas_call x1, Pallas kernels, branch(): pl.pallas_call(unpack_kernel, out_shape=jax.ShapeDtypeStruct((tokens, col...  13.4 us

commit v1 on v0

--- a/solution.py
+++ b/solution.py
@@ -12,27 +12,31 @@
 NB = 256
 HB = NB // 2
 KC = 3072
+XC = 1536
 BUCKETS = (352, 416, 448) + tuple(range(480, 673, 16)) + (704, 736, 784)
 PER = 2
-LAST = 7
+LAST = 6
 OFFS, LONE_TILE, LONE_ROW, LONE_SLOT, LONE_SOURCE, MERGE = 50, 54, 55, 56, 57, 64
 
 
-def fused_kernel(rows, table_ref, x_ref, w_ref, y_ref, xp, stage0, stage1, lone, wbuf, part, ra, sb, so, rb, out,
+def fused_kernel(rows, table_ref, x_ref, w_ref, y_ref, xp, stage0, stage1, stage2, stage3, lone, wbuf, part, ra, sb, so, rb, out,
                  xsem, wsem, send_a, recv_a, send_b, recv_b, send_c, recv_c, send_e, recv_e, send_d, recv_d, osem):
     depth, cols = w_ref.shape
     blocks = cols // NB
     half = rows // 2
-    stages = (stage0, stage1)
+    stages = (stage0, stage1, stage2, stage3)
+    ns = len(stages)
     me = lax.axis_index("tp")
     core = lax.rem(me, 2)
     chip = me // 2
     sibling = {"tp": me + 1 - 2 * core}
     peer = {"tp": lax.rem(me + 2, 4)}
     nk = depth // KC
-
-    def x_copy(k):
-        return pltpu.make_async_copy(x_ref.at[:, :, pl.ds(k * KC, KC)], stages[k % 2], xsem.at[k % 2])
+    nx = depth // XC
+    per = nx // nk
+
+    def x_copy(n):
+        return pltpu.make_async_copy(x_ref.at[:, :, pl.ds(n * XC, XC)], stages[n % ns], xsem.at[n % ns])
 
     def w_copy(b, k):
         s = lax.rem(b, 2)
@@ -66,38 +70,43 @@
         r = lax.rem(b, 8)
         return pltpu.make_async_copy(out.at[r], y_ref.at[b], osem.at[r])
 
-    x_copy(0).start()
-    w_copy(0, 0).start()
-    x_copy(1).start()
-    w_copy(0, 1).start()
+    for n in range(ns):
+        x_copy(n).start()
+        if n % per == per - 1:
+            w_copy(0, n // per).start()
 
     barrier = pltpu.get_barrier_semaphore()
     for other in (sibling, peer):
         pl.semaphore_signal(barrier, inc=1, device_id=other, device_id_type=MESH)
     pl.semaphore_wait(barrier, 2)
 
-    row = lax.broadcasted_iota(jnp.int32, (TILE, KC), 0)
-
-    def pack(k):
-        stage = stages[k % 2]
-        x_copy(k).wait()
+    row = lax.broadcasted_iota(jnp.int32, (TILE, XC), 0)
+
+    def pack(n):
+        stage = stages[n % ns]
+        x_copy(n).wait()
+        if n == nx - 1:
+            for k in range(nk):
+                w_copy(1, k).start()
         first = stage[table_ref[LONE_SOURCE]][0:1, :].astype(jnp.float32)
-        lone[...] = jnp.broadcast_to(first, (TILE, KC)).astype(lone.dtype)
+        lone[...] = jnp.broadcast_to(first, (TILE, XC)).astype(lone.dtype)
 
         def tile(t, carry):
             at = pl.ds(pl.multiple_of(t * TILE, TILE), TILE)
-            xp[at, k * KC:(k + 1) * KC] = jnp.where(row + 1 == table_ref[MERGE + t], lone[...], stage[table_ref[t]])
+            xp[at, n * XC:(n + 1) * XC] = jnp.where(row + 1 == table_ref[MERGE + t], lone[...], stage[table_ref[t]])
             return carry
 
         lax.fori_loop(0, rows // TILE, tile, 0)
-        if k + 2 < nk:
-            x_copy(k + 2).start()
-            w_copy(0, k + 2).start()
-        if k == nk - 1:
-            for j in range(nk):
-                w_copy(1, j).start()
-
-    def exchange(i):
+        if n + ns < nx:
+            x_copy(n + ns).start()
+            if (n + ns) % per == per - 1:
+                w_copy(0, (n + ns) // per).start()
+
+    def pack_for(k):
+        for n in range(k * per, (k + 1) * per):
+            pack(n)
+
+    def reduce_on(i):
         @pl.when(jnp.logical_and(i >= 1, i - 1 < blocks))
         def _():
             b = i - 1
@@ -109,37 +118,42 @@
             so[q] = part[s, core, here, :] + ra[s, here, :]
             copy_b(b).start()
 
-        @pl.when(jnp.logical_and(i >= 3, i - 3 < blocks))
-        def _():
-            b = i - 3
+    def finish(i):
+        @pl.when(jnp.logical_and(i >= 2, i - 2 < blocks))
+        def _():
+            b = i - 2
             copy_b(b).wait()
             out[lax.rem(b, 8), core, chip] = (so[lax.rem(b, 4)] + rb[lax.rem(b, 8)]).astype(out.dtype)
             copy_c(b).start()
             copy_e(b).start()
 
+        @pl.when(jnp.logical_and(i >= 4, i - 4 < blocks))
+        def _():
+            copy_c(i - 4).wait()
+            copy_d(i - 4).start()
+
         @pl.when(jnp.logical_and(i >= 5, i - 5 < blocks))
         def _():
-            copy_c(i - 5).wait()
-            copy_d(i - 5).start()
+            copy_e(i - 5).wait()
+            copy_d(i - 5).wait()
+            copy_o(i - 5).start()
 
         @pl.when(jnp.logical_and(i >= 6, i - 6 < blocks))
         def _():
-            copy_e(i - 6).wait()
-            copy_d(i - 6).wait()
-            copy_o(i - 6).start()
-
-        @pl.when(jnp.logical_and(i >= 7, i - 7 < blocks))
-        def _():
-            copy_o(i - 7).wait()
+            copy_o(i - 6).wait()
 
     def step(j, carry):
         i, k = j // nk, lax.rem(j, nk)
         for early in range(nk):
-            pl.when(j == early)(functools.partial(pack, early))
-
-        @pl.when(k == jnp.where(i == 1, 1, 2))
-        def _():
-            exchange(i)
+            pl.when(j == early)(functools.partial(pack_for, early))
+
+        @pl.when(k == jnp.where(i <= 3, 1, 2))
+        def _():
+            reduce_on(i)
+
+        @pl.when(k == nk - 1)
+        def _():
+            finish(i)
 
         @pl.when(i < blocks)
         def _():
@@ -253,9 +267,8 @@
         out_specs=pl.BlockSpec(memory_space=pl.ANY),
         scratch_shapes=[
             pltpu.VMEM((rows, depth), bf16),
-            pltpu.VMEM((tokens // TILE, TILE, KC), bf16),
-            pltpu.VMEM((tokens // TILE, TILE, KC), bf16),
-            pltpu.VMEM((TILE, KC), bf16),
+            *[pltpu.VMEM((tokens // TILE, TILE, XC), bf16)] * 4,
+            pltpu.VMEM((TILE, XC), bf16),
             pltpu.VMEM((2, depth, NB), bf16),
             pltpu.VMEM((2, 2, rows, HB), f32),
             pltpu.VMEM((2, rows, HB), f32),
@@ -263,7 +276,7 @@
             pltpu.VMEM((4, half, HB), f32),
             pltpu.VMEM((8, half, HB), f32),
             pltpu.VMEM((8, 2, 2, half, HB), bf16),
-            dma((2,)), dma((2, depth // KC)), dma((2,)), dma((2,)), dma((4,)), dma((8,)),
+            dma((4,)), dma((2, depth // KC)), dma((2,)), dma((2,)), dma((4,)), dma((8,)),
             dma((8,)), dma((8,)), dma((8,)), dma((8,)), dma((8,)), dma((8,)), dma((8,)),
         ],
         compiler_params=pltpu.CompilerParams(collective_id=index, has_side_effects=True, vmem_limit_bytes=66_000_000),
@@ -288,38 +301,61 @@
     )(lengths, table, packed)
 
 
+def table_kernel(tokens, lens_ref, table_ref, index_ref):
+    slots = lens_ref.shape[0]
+    slot_tiles = tokens // slots // TILE
+    lens = [lens_ref[s] for s in range(slots)]
+    lone = jnp.int32(slots - 1)
+    for s in reversed(range(slots - 1)):
+        lone = jnp.where(lens[s] == 1, s, lone)
+    rest = [lax.rem(lens[s], TILE) for s in range(slots)]
+    host = jnp.int32(-1)
+    for s in reversed(range(slots)):
+        host = jnp.where(jnp.logical_and(lone != s, rest[s] != 0), s, host)
+    offs, total = [], jnp.int32(0)
+    lone_tile, lone_row = jnp.int32(0), jnp.int32(0)
+    for s in range(slots):
+        offs.append(total)
+        tiles = jnp.where(jnp.logical_and(host >= 0, lone == s), 0, lax.div(lens[s] + (TILE - 1), TILE))
+        total = total + tiles
+        lone_tile = jnp.where(host == s, total, lone_tile)
+        lone_row = jnp.where(host == s, rest[s], lone_row)
+
+    def tile(t, carry):
+        source = t
+        for s in range(1, slots):
+            source = jnp.where(t >= offs[s], s * slot_tiles + t - offs[s], source)
+        table_ref[t] = jnp.where(t < total, source, 0)
+        table_ref[MERGE + t] = jnp.where(t + 1 == lone_tile, lone_row + 1, 0)
+        return carry
+
+    lax.fori_loop(0, OFFS, tile, 0)
+    for s in range(slots):
+        table_ref[OFFS + s] = offs[s]
+    table_ref[LONE_TILE] = lone_tile
+    table_ref[LONE_ROW] = lone_row
+    table_ref[LONE_SLOT] = lone
+    table_ref[LONE_SOURCE] = lone * slot_tiles
+    index = jnp.int32(0)
+    for size in BUCKETS[:-1]:
+        index = index + (total * TILE > size).astype(jnp.int32)
+    index_ref[0] = index
+
+
 def make_table(lengths, tokens):
-    slots = lengths.shape[0]
-    slot_tiles = tokens // slots // TILE
-    slot = jnp.arange(slots, dtype=jnp.int32)
-    ahead = slot[None, :] < slot[:, None]
-
-    def first(flags):
-        return flags & ~jnp.any(ahead & flags[None, :], axis=1)
-
-    lone = first(lengths == 1)
-    rest = lax.rem(lengths, TILE)
-    free = (rest != 0) & ~lone
-    host = first(free)
-    merged = lone & jnp.any(free[None, :] & (slot[:, None] >= 0), axis=1)
-    tiles = jnp.where(merged, 0, lax.div(lengths + (TILE - 1), TILE))
-    offs = jnp.sum(jnp.where(ahead, tiles[None, :], 0), axis=1)
-    ends = offs + tiles
-    place = jnp.arange(128, dtype=jnp.int32)[:, None]
-    cells = jnp.where((place >= offs) & (place < ends), slot * slot_tiles + place - offs, 0)
-    cells += jnp.where(place == OFFS + slot, offs, 0)
-    cells += jnp.where((place == LONE_TILE) & host, ends, 0)
-    cells += jnp.where((place == LONE_ROW) & host, rest, 0)
-    cells += jnp.where((place == LONE_SLOT) & lone, slot, 0)
-    cells += jnp.where((place == LONE_SOURCE) & lone, slot * slot_tiles, 0)
-    cells += jnp.where((place - MERGE == ends - 1) & host, rest + 1, 0)
-    return jnp.sum(cells, axis=1), jnp.sum(tiles)
+    smem = pl.BlockSpec(memory_space=pltpu.SMEM)
+    return pl.pallas_call(
+        functools.partial(table_kernel, tokens),
+        out_shape=(jax.ShapeDtypeStruct((128,), jnp.int32), jax.ShapeDtypeStruct((1,), jnp.int32)),
+        in_specs=[smem],
+        out_specs=(smem, smem),
+        name="table",
+    )(lengths)
 
 
 def solution(mesh):
     def local_part(x_loc, w_loc, lengths):
-        table, total = make_table(lengths, x_loc.shape[0])
-        index = jnp.sum((total * TILE > jnp.array(BUCKETS[:-1], jnp.int32)).astype(jnp.int32))
-        return lax.switch(index, [functools.partial(branch, j, rows) for j, rows in enumerate(BUCKETS)], x_loc, w_loc, lengths, table)
+        table, index = make_table(lengths, x_loc.shape[0])
+        return lax.switch(index[0], [functools.partial(branch, j, rows) for j, rows in enumerate(BUCKETS)], x_loc, w_loc, lengths, table)
 
     return jax.shard_map(local_part, mesh=mesh, in_specs=(P("data", "tp"), P("tp", None), P("data")), out_specs=P("data", None), check_vma=False)

time: 271 us -> 248 us (0.915); the launches traced: 268 us -> 248 us
  Pallas kernels: 259 us -> 246 us
  other arithmetic: 6.2 us -> 0 us
    pallas_call x1, Pallas kernels: 245 us -> 231 us  [branch(): pl.pallas_call(functools.partial(fused_kernel, rows), out_shape=jax.Shape...]
    reduce_sum x4 -> x0, other arithmetic: 3.96 us -> none  [the longest x2 2.55 us: make_table(): return (jnp.sum(cells, axis=1), jnp.sum(tiles))]
where the time goes in v1:
time: 248 us
  Pallas kernels  246 us (99%)
    pallas_call x1, Pallas kernels, branch(): pl.pallas_call(functools.partial(fused_kernel, rows), out_shape=jax.Shape...  231 us
    pallas_call x1, Pallas kernels, branch(): pl.pallas_call(unpack_kernel, out_shape=jax.ShapeDtypeStruct((tokens, col...  13 us

profile of v1, /device:TPU:0, one launch (start us, length us, event | category | flops | bytes accessed | tf_op | source)
XLA Modules:
  0.0 247.6 jit_solution(12737957816829636133)
XLA Ops:
  0.0 1.8 table.1
  2.4 245.0 %conditional.1 = (bf16[1024,12288]{1,0:T(8,128)(2,1)}) conditional(s32[]{:T(128)} %bitcast.38, (bf16[1024,12288]{1,0:T(8,128)(2,1)}, s32[128]{0:T(128)S(1)}, bf16[12288,12288]{1,0:T(8,128)(2,1)}, s32[4]{0:T(128)}) %tuple.62, (bf16[1024,12288]{1,0:T(8,128)(2,1)}, s32[128]{0:T(128)S(1)}, ...), branch_computations={%region_0.0_spmd, %region_1.0_spmd, %region_2.0_spmd, %region_3.0_... | conditional | flops 236760072192 | bytes 346423392 | solution.py:359
  2.5 0.0 copy-start.6
  2.5 231.4 %fused_528.1 = bf16[48,2,2,264,128]{4,3,2,1,0:T(8,128)(2,1)} custom-call(s32[128]{0:T(128)S(1)} %get-tuple-element.202.table_ref, bf16[64,16,12288]{2,1,0:T(8,128)(2,1)} %bitcast.64, bf16[12288,12288]{1,0:T(8,128)(2,1)} %get-tuple-element.321.w_ref), custom_call_target="tpu_custom_call" | custom-call | flops 159450660864 | bytes 301989888 | tf_op jit(solution)/shard_map/cond/branch_6_fun/fused_528/pallas_call | solution.py:263
  233.9 0.0 copy-done.6
  233.9 13.0 %unpack_528.1 = bf16[1024,12288]{1,0:T(8,128)(2,1)} custom-call(s32[4]{0:T(128)S(1)} %copy-done.6, s32[128]{0:T(128)S(1)} %get-tuple-element.202.table_ref, bf16[48,2,528,128]{3,2,1,0:T(8,128)(2,1)} %bitcast.51), custom_call_target="tpu_custom_call" | custom-call | bytes 38141952 | tf_op jit(solution)/shard_map/cond/branch_6_fun/unpack_528/pallas_call | solution.py:288
Async XLA Ops:
  2.5 231.4 %copy-start.6 = (s32[4]{0:T(128)S(1)}, s32[4]{0:T(128)}, u32[]{:S(2)}) copy-start(s32[4]{0:T(128)} %get-tuple-element.201.lens_ref) | copy-start | bytes 52 | tf_op jit(solution)/shard_map/cond
